TPU v7x, 32 devices: a whole 2x2x4 slice. The times are simulated.
32 devices in a mesh: leaf: 16 (over z, y, x), sep: 2 (over core).
Axes of the slice: x: 2, y: 2, z: 4, core: 2. Of those that a mesh axis runs over, the one named last changes fastest.
Arguments:
- leaf_rhs: bfloat16 [16, 256, 2048], P('leaf', None, 'sep'), may hold values from -6 to 6
- leaf_inv: bfloat16 [16, 2048, 2048], P('leaf', 'sep'), may hold values from -0.125 to 0.125
- leaf_couple: bfloat16 [16, 512, 2048], P('leaf', None, 'sep'), may hold values from -0.0625 to 0.0625
- sep_rhs: float32 [16, 256, 512], P('leaf', None, 'sep'), may hold values from -6 to 6
- sep_inv: float32 [16, 512, 512], P('leaf', 'sep'), may hold values from -0.25 to 0.25
- sep_couple: float32 [16, 512, 512], P('leaf', None, 'sep'), may hold values from -0.1875 to 0.1875
Outputs:
- leaf_solution: float32 [16, 256, 2048], P('leaf', None, 'sep')
- sep_solution: float32 [16, 256, 512], P('leaf', None, 'sep')
All inputs are finite; a program needn't handle non-finite values.
Results may differ from a plain program's by a relative error of at most 0.0042.
Values may be sent and summed in bfloat16 or wider, within the bound.
A program may use at most 128 MiB of HBM per device.

v0:
```python
import functools

import jax
import jax.numpy as jnp
from jax import lax
from jax.experimental import pallas as pl
from jax.experimental.pallas import tpu as pltpu
from jax.sharding import PartitionSpec as P

F32 = jnp.float32
BF16 = jnp.bfloat16


def dot_nt(a, b):
    return lax.dot_general(a, b, (((1,), (1,)), ((), ())), preferred_element_type=F32)


def dot_nn(a, b):
    return lax.dot_general(a, b, (((1,), (0,)), ((), ())), preferred_element_type=F32)


def dot_tn(a, b):
    return lax.dot_general(a, b, (((0,), (0,)), ((), ())), preferred_element_type=F32)


def halves(value):
    high = value.astype(BF16)
    return high, (value - high.astype(F32)).astype(BF16)


def three_pass(a, b, dot):
    ah, al = halves(a)
    bh, bl = halves(b)
    return dot(ah, bh) + (dot(ah, bl) + dot(al, bh))


def two_pass(a, b, dot):
    rows = a.shape[0]
    both = dot(jnp.concatenate(halves(a), axis=0), b)
    return both[:rows] + both[rows:]


def kernel(
    leaves,
    rhs_ref, inv_hbm, couple_hbm, srhs_ref, sinv_ref, scpl_ref,
    leaf_out, sep_out,
    inv, couple, other_rhs, state, other_inv, other_cpl, fac, top,
    r1, rb, rt, part_send, part_own, part_recv, xs, xr, o1, yr,
    ys, zs, zb, zr, sols, sb, dn, s2, s1, sh, gath, fin_s, fin_r, sep_acc,
    load_sem, send_sem, recv_sem, fsend, frecv, rsend, rrecv, osend, orecv, gsend, grecv, tsend, trecv,
):
    p = lax.axis_index("leaf")
    c = lax.axis_index("sep")
    oc = 1 - c
    b0 = p % 2
    b1 = (p // 2) % 2
    q = p // 4
    planes = leaves // 4
    below_top = planes // 2 - 1
    xp = p + 1 - 2 * b0
    yp = p + 2 - 4 * b1
    rows = rhs_ref.shape[0]
    part = rhs_ref.shape[1]
    width = sinv_ref.shape[1]
    half = width // 2
    quarter = rows // 4
    eighth = rows // 8

    loads = [
        pltpu.make_async_copy(couple_hbm.at[0], couple, load_sem.at[0]),
        pltpu.make_async_copy(inv_hbm.at[0], inv, load_sem.at[1]),
    ]
    for copy in loads:
        copy.start()

    me = p * 2 + c
    count = 2 * leaves
    barrier = pltpu.get_barrier_semaphore()

    @pl.loop(1, count)
    def _(step):
        to = (me + step) % count
        pl.semaphore_signal(barrier, inc=1, device_id=(to // 2, to % 2), device_id_type=pl.DeviceIdType.MESH)

    pl.semaphore_wait(barrier, count - 1)

    pending = []

    def remote(src, dst, ssem, rsem, to):
        return pltpu.make_async_remote_copy(
            src_ref=src, dst_ref=dst, send_sem=ssem, recv_sem=rsem,
            device_id=to, device_id_type=pl.DeviceIdType.MESH,
        )

    def when(cond, action):
        if cond is None:
            action()
        else:
            @pl.when(cond)
            def _():
                action()

    def push(src, dst, ssem, rsem, to, cond=None):
        copy = remote(src, dst, ssem, rsem, to)
        when(cond, lambda: copy.start())
        pending.append((cond, copy))

    def arrive(dst, rsem, cond=None):
        copy = remote(dst, dst, send_sem.at[0], rsem, (p, oc))
        when(cond, lambda: copy.wait_recv())

    def send(src, dst, slot, to, cond=None):
        push(src, dst, send_sem.at[slot], recv_sem.at[slot], to, cond)

    def got(dst, slot, cond=None):
        arrive(dst, recv_sem.at[slot], cond)

    mate = (p, oc)
    send(sinv_ref, other_inv, 1, mate)
    send(scpl_ref.at[pl.ds(pl.multiple_of(oc * half, half), half)], other_cpl, 2, mate)
    send(rhs_ref, other_rhs, 0, mate)

    is_even = b0 == 0
    is_top = p == leaves - 1
    for t in range(4):
        tc, tb0 = t // 2, t % 2
        to = (p - b0 + tb0, tc)
        mine = (c == tc) & (b0 == tb0)
        push(
            srhs_ref.at[pl.ds(t * quarter, quarter)], r1.at[c], rsend.at[t], rrecv.at[c],
            to, is_even & jnp.logical_not(mine),
        )

        @pl.when(is_even & mine)
        def _():
            r1[c] = srhs_ref[pl.ds(t * quarter, quarter), :]

    is_odd = (b0 == 1) & jnp.logical_not(is_top)
    for t in range(8):
        tc, tb0, tb1 = t // 4, (t // 2) % 2, t % 2
        to = (4 * q + 2 * tb1 + tb0, tc)
        mine = (c == tc) & (b0 == tb0) & (b1 == tb1)
        block = srhs_ref.at[pl.ds(t * eighth, eighth)]
        push(block, rb.at[b1, c], rsend.at[4 + t], rrecv.at[2 + 2 * b1 + c], to, is_odd & jnp.logical_not(mine))

        @pl.when(is_odd & mine)
        def _():
            rb[b1, c] = srhs_ref[pl.ds(t * eighth, eighth), :]

        to = (4 * below_top + 2 * tb1 + tb0, tc)
        push(block, rt.at[c], rsend.at[12 + t], rrecv.at[6 + c], to, is_top)

    own = b0 * (1 + b1)
    got(other_inv, 1)
    got(other_cpl, 2)
    at = pl.ds(pl.multiple_of(c * half, half), half)
    ours = scpl_ref[at, :]

    def n_rows():
        mine, other = sinv_ref[:, at], other_inv[:, at]
        return (three_pass(mine, sinv_ref[...], dot_tn) + three_pass(other, other_inv[...], dot_tn)).astype(BF16)

    @pl.when(is_top)
    def _():
        fac[0, own, c] = n_rows()

    @pl.when(jnp.logical_not(is_top))
    def _():
        m_rows = three_pass(ours, sinv_ref[...], dot_nn) + three_pass(other_cpl[...], other_inv[...], dot_nn)
        fac[0, own, c] = m_rows.astype(BF16)

    theirs = (1 - b0) * (1 + b1)
    across = 2 - b1

    chunk = half // 4
    last = q == planes - 1
    joint = q == below_top
    place = p % 4

    def top_share(i, cond):
        span = pl.ds(i * chunk, chunk)
        push(
            fac.at[0, 2, c, span], top.at[c, span], tsend.at[i], trecv.at[i],
            (4 * below_top + place, c), last & cond,
        )

    def share(kind, idx, path, i, to, cond=None):
        ref = fac.at[kind, idx, c, pl.ds(i * chunk, chunk)]
        push(ref, ref, fsend.at[kind, path, i], frecv.at[kind, 1 if path == 4 else path, i], to, cond)

    def shared(kind, idx, core, path, i, cond=None):
        arrive(fac.at[kind, idx, core, pl.ds(i * chunk, chunk)], frecv.at[kind, path, i], cond)

    def factor_x(kind):
        for i in range(4):
            share(kind, own, 0, i, (xp, c))
            if kind == 0:
                share(kind, own, 1, i, (yp, c), b0 == 1)
                top_share(i, (b0 == 1) & (b1 == 1))
        ref = fac.at[kind, own, c]
        send(ref, ref, 3 + kind, mate)

    def factor_y(kind):
        for i in range(4):
            shared(kind, theirs, c, 0, i)
            share(kind, theirs, 4, i, (yp, c), b0 == 0)
            share(kind, theirs, 2, i, mate)
            if kind == 0:
                top_share(i, (b0 == 0) & (b1 == 1))

    def factor_end(kind, cond=None):
        for i in range(4):
            shared(kind, across, c, 1, i, cond)
            share(kind, across, 3, i, mate, cond)

    def factor_wait(kind, which):
        if which == 0:
            got(fac.at[kind, own, oc], 3 + kind)
        else:
            for i in range(4):
                shared(kind, (theirs, across)[which - 1], oc, 1 + which, i)

    def factor(kind, idx):
        return fac[kind, idx].reshape(width, width)

    factor_x(0)
    fac[1, own, c] = n_rows()

    got(other_rhs, 0)
    loads[1].wait()
    mine_cols = pl.ds(pl.multiple_of(c * part, part), part)
    other_cols = pl.ds(pl.multiple_of(oc * part, part), part)
    piece = part // 4
    for j in range(4):
        at_j = pl.ds(j * piece, piece)
        value = dot_nt(rhs_ref[...], inv[at_j, mine_cols]) + dot_nt(other_rhs[...], inv[at_j, other_cols])
        state[:, at_j] = value.astype(BF16)
    loads[0].wait()
    mid = rows // 2
    part_send[...] = dot_nt(
        state[pl.ds(pl.multiple_of(oc * mid, mid), mid), :], couple[...]
    ).reshape(2, quarter, width)
    send(part_send, part_recv, 13, mate)
    part_own[...] = dot_nt(
        state[pl.ds(pl.multiple_of(c * mid, mid), mid), :], couple[...]
    ).reshape(2, quarter, width)
    got(part_recv, 13)
    xs[...] = (part_own[1 - b0] + part_recv[1 - b0]).astype(BF16)
    send(xs, xr, 14, (xp, c))
    factor_x(1)
    factor_y(0)
    factor_end(0, b0 == 1)
    for i in range(4):
        top_share(i, (b0 == 1) & (b1 == 0))
    factor_wait(0, 0)
    factor_wait(0, 1)

    for h in range(2):
        arrive(r1.at[h], rrecv.at[h], jnp.logical_not(is_even & (c == h)))
    got(xr, 14)
    taken = part_own[b0] + part_recv[b0] + xr[...].astype(F32)
    w1 = jnp.concatenate([r1[0], r1[1]], axis=1) - taken
    o1[...] = two_pass(w1, factor(0, 0), dot_nt).reshape(2, eighth, width)
    ys[...] = o1[1 - b1].astype(BF16)
    send(ys, yr, 15, (yp, c))
    for i in range(4):
        share(1, own, 1, i, (yp, c), b0 == 1)
    factor_end(0, b0 == 0)
    factor_wait(0, 2)

    for h in range(2):
        arrive(rb.at[0, h], rrecv.at[2 + h], jnp.logical_not((b0 == 1) & (b1 == 0) & (c == h)))
    got(yr, 15)
    w2 = jnp.concatenate([rb[0, 0], rb[0, 1]], axis=1) - (o1[b1] + yr[...].astype(F32))
    out2 = two_pass(w2, factor(0, 1), dot_nt)
    even_plane = q % 2 == 0
    odd_plane = jnp.logical_not(even_plane)
    zs[0] = out2
    zb[0] = out2.astype(BF16)
    send(zb.at[0], zr.at[1], 19, (4 * (q - 1) + place, c), odd_plane)
    for i in range(4):
        top_share(i, (b0 == 0) & (b1 == 0))

    reach = 1
    for bit in range(leaves.bit_length()):
        reach = jnp.where((q + 1) % (2 ** (bit + 1)) == 0, 2 ** (bit + 1), reach)
    upper = (q // (2 * reach)) % 2 == 1
    parent = jnp.where(upper, q - reach, q + reach)
    has_node = jnp.logical_not(last)
    low_child = q - reach // 2
    high_child = q + reach // 2
    inner = odd_plane & has_node

    factor_y(1)
    for i in range(4):
        arrive(top.at[c, pl.ds(i * chunk, chunk)], trecv.at[i], joint)
    send(top.at[c], top.at[c], 17, mate, joint)

    for h in range(2):
        arrive(rb.at[1, h], rrecv.at[4 + h], has_node & jnp.logical_not((b0 == 1) & (b1 == 1) & (c == h)))
    got(zr.at[0], 18, inner)
    got(zr.at[1], 19, has_node)
    w3_at = s2.at[0]

    @pl.when(has_node)
    def _():
        first = jnp.where(even_plane, zs[0], zr[0].astype(F32))
        w3 = jnp.concatenate([rb[1, 0], rb[1, 1]], axis=1) - (first + zr[1].astype(F32))
        w3_at[...] = w3
        out3 = two_pass(w3, factor(0, 2), dot_nt)
        zs[1] = out3
        zb[1] = out3.astype(BF16)

    climbs = has_node & jnp.logical_not(joint)
    up_slot = 18 + jnp.where(upper, 1, 0)
    push(
        zb.at[1], zr.at[jnp.where(upper, 1, 0)], send_sem.at[20], recv_sem.at[up_slot],
        (4 * parent + place, c), climbs,
    )

    factor_end(1)
    for h in range(2):
        arrive(rt.at[h], rrecv.at[6 + h], joint)
    got(top.at[oc], 17, joint)

    @pl.when(joint)
    def _():
        wt = jnp.concatenate([rt[0], rt[1]], axis=1) - zs[1]
        sols[0] = two_pass(wt, top[...].reshape(width, width), dot_nn)
    for which in range(3):
        factor_wait(1, which)

    w3n = two_pass(jnp.where(has_node, w3_at[...], 0.0), factor(1, 2), dot_nn)
    got(dn.at[0], 21, climbs)

    @pl.when(has_node)
    def _():
        above = jnp.where(joint, sols[0], dn[0].astype(F32))
        sol3 = w3n - two_pass(above, factor(0, 2), dot_nn)
        sols[1] = sol3
        sb[...] = sol3.astype(BF16)

    push(sb, dn.at[0], send_sem.at[22], recv_sem.at[21], (4 * low_child + place, c), inner)
    push(sb, dn.at[0], send_sem.at[23], recv_sem.at[21], (4 * high_child + place, c), inner)
    push(sb, dn.at[1], send_sem.at[24], recv_sem.at[22], (4 * (q + 1) + place, c), even_plane)
    w2n = two_pass(w2, factor(1, 1), dot_nn)
    w1n = two_pass(w1, factor(1, 0), dot_nn)
    got(dn.at[1], 22, odd_plane)
    above2 = jnp.where(even_plane, sb[...], dn[1])
    sol2 = w2n - dot_nn(above2, factor(0, 1))
    s1[...] = sol2
    sh[b1] = sol2.astype(BF16)
    send(sh.at[b1], sh.at[b1], 25, (yp, c))
    got(sh.at[1 - b1], 25)
    sol1 = w1n - dot_nn(sh[...].reshape(quarter, width), factor(0, 0))
    s2[...] = sol1.reshape(2, eighth, width)
    slot = c * 2 + b0
    gath[slot] = sol1.astype(BF16)
    for t in range(1, 4):
        to_c = (c + t // 2) % 2
        to_b = (b0 + t % 2) % 2
        push(
            gath.at[slot], gath.at[slot], osend.at[t], orecv.at[t], (p - b0 + to_b, to_c),
        )

    block8 = c * 4 + b0 * 2 + b1
    for h in range(2):
        cols = pl.ds(h * half, half)
        for part_at in range(2):
            block = 2 * slot + part_at
            to = (p - b0, h)
            mine = is_even & (c == h)
            push(
                s2.at[part_at, :, cols], sep_acc.at[block], osend.at[4 + 2 * h + part_at],
                orecv.at[4 + block], to, jnp.logical_not(mine),
            )

            @pl.when(mine)
            def _():
                sep_acc[block] = s2[part_at, :, cols]

        here = (b0 == 1) & (b1 == 0) & (c == h)
        push(s1.at[:, cols], sep_acc.at[block8], osend.at[8 + h], orecv.at[4 + block8], (4 * q + 1, h), jnp.logical_not(here))

        @pl.when(here)
        def _():
            sep_acc[block8] = s1[:, cols]

        here = (b0 == 1) & (b1 == 1) & (c == h)
        push(sols.at[1, :, cols], sep_acc.at[block8], osend.at[10 + h], orecv.at[4 + block8], (4 * q + 3, h), has_node & jnp.logical_not(here))

        @pl.when(here & has_node)
        def _():
            sep_acc[block8] = sols[1, :, cols]

        push(sols.at[0, :, cols], sep_acc.at[block8], osend.at[12 + h], orecv.at[4 + block8], (leaves - 1, h), joint)

    def gathered(t):
        from_c = (c + t // 2) % 2
        from_b = (b0 + t % 2) % 2
        arrive(gath.at[from_c * 2 + from_b], orecv.at[t])

    def backward(group, side):
        spans = [pl.ds(pl.multiple_of((2 * h + side) * quarter, quarter), quarter) for h in range(2)]
        whole = jnp.concatenate([gath[side], gath[2 + side]], axis=0)
        before = jnp.concatenate([state[spans[0], :], state[spans[1], :]], axis=0).astype(F32)
        residue = (before - dot_nn(whole, couple[...])).astype(BF16)
        for j in range(4):
            cols = pl.ds(pl.multiple_of(oc * part + j * piece, piece), piece)
            fin_s[group, j] = dot_nn(residue, inv[:, cols]).astype(BF16)
            push(fin_s.at[group, j], fin_r.at[group, j], gsend.at[group, j], grecv.at[group, j], mate)
        for j in range(4):
            cols = pl.ds(pl.multiple_of(c * part + j * piece, piece), piece)
            value = dot_nn(residue, inv[:, cols])
            for h in range(2):
                leaf_out[spans[h], pl.ds(j * piece, piece)] = value[h * quarter:(h + 1) * quarter]
        return spans

    gathered(2)
    spans = [backward(0, b0)]
    gathered(1)
    gathered(3)
    spans.append(backward(1, 1 - b0))
    for group in range(2):
        for j in range(4):
            arrive(fin_r.at[group, j], grecv.at[group, j])
            for h in range(2):
                leaf_out[spans[group][h], pl.ds(j * piece, piece)] += fin_r[group, j, pl.ds(h * quarter, quarter)].astype(F32)

    for block in range(8):
        bc, bb0, bb1 = block // 4, (block // 2) % 2, block % 2
        self_even = is_even & (c == bc) & (bb0 == 0)
        self_odd = (b0 == 1) & jnp.logical_not(is_top) & (c == bc) & (bb0 == 1) & (b1 == bb1)
        arrive(sep_acc.at[block], orecv.at[4 + block], jnp.logical_not(self_even | self_odd))
    sep_out[...] = sep_acc[...].reshape(rows, half)

    for cond, copy in pending:
        when(cond, lambda copy=copy: copy.wait_send())


def local(leaves, leaf_rhs, leaf_inv, leaf_couple, sep_rhs, sep_inv, sep_couple):
    _, rows, part = leaf_rhs.shape
    full = leaf_inv.shape[2]
    width = sep_inv.shape[2]
    half = width // 2
    quarter, eighth = rows // 4, rows // 8
    vmem = pl.BlockSpec(memory_space=pltpu.VMEM)
    anywhere = pl.BlockSpec(memory_space=pl.ANY)
    V = pltpu.VMEM
    dma = pltpu.SemaphoreType.DMA
    leaf_solution, sep_solution = pl.pallas_call(
        functools.partial(kernel, leaves),
        out_shape=(pltpu.VMEM((rows, part), F32), pltpu.VMEM((rows, half), F32)),
        in_specs=[vmem, anywhere, anywhere, vmem, vmem, vmem],
        out_specs=(vmem, vmem),
        scratch_shapes=[
            V((part, full), BF16), V((width, part), BF16), V((rows, part), BF16), V((rows, part), BF16),
            V((half, width), F32), V((half, half), F32), V((2, 3, 2, half, width), BF16), V((2, half, width), BF16),
            V((2, quarter, half), F32), V((2, 2, eighth, half), F32), V((2, eighth, half), F32),
            V((2, quarter, width), F32), V((2, quarter, width), F32), V((2, quarter, width), F32),
            V((quarter, width), BF16), V((quarter, width), BF16), V((2, eighth, width), F32), V((eighth, width), BF16),
            V((eighth, width), BF16), V((2, eighth, width), F32), V((2, eighth, width), BF16), V((2, eighth, width), BF16),
            V((2, eighth, width), F32), V((eighth, width), BF16), V((2, eighth, width), BF16), V((2, eighth, width), F32),
            V((eighth, width), F32), V((2, eighth, width), BF16), V((4, quarter, width), BF16),
            V((2, 4, rows // 2, part // 4), BF16), V((2, 4, rows // 2, part // 4), BF16), V((8, eighth, half), F32),
            dma((2,)), dma((30,)), dma((30,)), dma((2, 5, 4)), dma((2, 5, 4)), dma((20,)), dma((8,)), dma((14,)), dma((12,)),
            dma((2, 4)), dma((2, 4)), dma((4,)), dma((4,)),
        ],
        compiler_params=pltpu.CompilerParams(
            collective_id=0, has_side_effects=True, vmem_limit_bytes=60 * 1024 * 1024
        ),
    )(leaf_rhs[0], leaf_inv, leaf_couple, sep_rhs[0], sep_inv[0], sep_couple[0])
    return leaf_solution[None], sep_solution[None]


def solution(mesh):
    return jax.shard_map(
        functools.partial(local, mesh.shape["leaf"]),
        mesh=mesh,
        in_specs=(
            P("leaf", None, "sep"),
            P("leaf", "sep", None),
            P("leaf", None, "sep"),
            P("leaf", None, "sep"),
            P("leaf", "sep", None),
            P("leaf", None, "sep"),
        ),
        out_specs=(P("leaf", None, "sep"), P("leaf", None, "sep")),
        check_vma=False,
    )
```

profile of v0, /device:TPU:31, one launch (start us, length us, event | category | flops | bytes accessed | tf_op | source)
XLA Modules:
  0.0 50.3 jit_solution(6534874592717111331)
XLA Ops:
  0.6 48.0 %shard_map.77 = (f32[256,1024]{1,0:T(8,128)S(1)}, f32[256,256]{1,0:T(8,128)S(1)}) custom-call(bf16[256,1024]{1,0:T(8,128)(2,1)} %bitcast.8, bf16[1,1024,2048]{2,1,0:T(8,128)(2,1)} %inv_hbm.1, bf16[1,512,1024]{2,1,0:T(8,128)(2,1)} %couple_hbm.1, f32[256,256]{1,0:T(8,128)} %bitcast.11, f32[256,512]{1,0:T(8,128)} %bitcast.9, f32[512,256]{1,0:T(8,128)} %bitcast.10), custom_call_target="tpu_custom_call" | custom-call | tf_op jit(solution)/shard_map/pallas_call | solution.py:451
  48.7 1.0 %copy.10 = f32[1,256,1024]{2,1,0:T(8,128)} copy(f32[1,256,1024]{2,1,0:T(8,128)S(1)} %bitcast.6) | data formatting | bytes 2097152
  49.6 0.7 %copy.11 = f32[1,256,256]{2,1,0:T(8,128)} copy(f32[1,256,256]{2,1,0:T(8,128)S(1)} %bitcast.7) | data formatting | bytes 524288
where the time goes:
time: 51.3 us; the launch traced here: 50.3 us
  Pallas kernels  48 us (94%)
  local copies, waits for them, and re-layouts  1.67 us (3%)
  between operations  0.64 us (1%)
    pallas_call x1, Pallas kernels, local(): pl.pallas_call(functools.partial(kernel, leaves), out_shape=(pltpu.VMEM((...  48 us
    unnamed x2, local copies, waits for them, and re-layouts  1.67 us

commit v1 on v0

v1 whole, which is shorter than its diff:
```python
import functools

import jax
import jax.numpy as jnp
from jax import lax
from jax.experimental import pallas as pl
from jax.experimental.pallas import tpu as pltpu
from jax.sharding import PartitionSpec as P

F32 = jnp.float32
BF16 = jnp.bfloat16
CHUNKS = 4
RECEIVES = 68


def dot_nt(a, b):
    return lax.dot_general(a, b, (((1,), (1,)), ((), ())), preferred_element_type=F32)


def dot_nn(a, b):
    return lax.dot_general(a, b, (((1,), (0,)), ((), ())), preferred_element_type=F32)


def dot_tn(a, b):
    return lax.dot_general(a, b, (((0,), (0,)), ((), ())), preferred_element_type=F32)


def halves(value):
    high = value.astype(BF16)
    return high, (value - high.astype(F32)).astype(BF16)


def three_pass(a, b, dot):
    ah, al = halves(a)
    bh, bl = halves(b)
    return dot(ah, bh) + (dot(ah, bl) + dot(al, bh))


def two_pass(a, b, dot):
    rows = a.shape[0]
    both = dot(jnp.concatenate(halves(a), axis=0), b)
    return both[:rows] + both[rows:]


def scope(name):
    return jax.named_scope(name)


def kernel(
    leaves,
    rhs_hbm, inv_hbm, couple_hbm, srhs_hbm, sinv_hbm, scpl_hbm,
    leaf_out, sep_out,
    rhs, inv, couple, srhs, sinv, scpl, other_rhs, state,
    parts, part_in, fac, top, srows, rb, rp, rt,
    out_send, out_own, out_in, base, xs, xr, w1s, o1, ys, yr,
    zb, zr, w2s, w3s, w4s, sols, sb, dn, w1g, sg, s2, s3, s4, st,
    fin_s, fin_r, sep_acc,
    load_sem, send_sem, recv_sem,
):
    p = lax.axis_index("leaf")
    c = lax.axis_index("sep")
    oc = 1 - c
    b0 = p % 2
    b1 = (p // 2) % 2
    q = p // 4
    place = p % 4
    planes = leaves // 4
    below_top = planes // 2 - 1
    xp = p + 1 - 2 * b0
    yp = p + 2 - 4 * b1
    mate = (p, oc)
    rows = rhs.shape[0]
    part = rhs.shape[1]
    width = sinv.shape[1]
    half = width // 2
    mid = rows // 2
    quarter = rows // 4
    eighth = rows // 8
    chunk = half // CHUNKS

    left, right = b0 == 0, b0 == 1
    near, far = b1 == 0, b1 == 1
    even_plane = q % 2 == 0
    odd_plane = jnp.logical_not(even_plane)
    last = q == planes - 1
    joint = q == below_top
    is_top = p == leaves - 1
    node = odd_plane & jnp.logical_not(last)
    fourth = q % 4 == 1
    pair_plane = q + 1 - 2 * (q % 2)
    reach = 1
    for bit in range(leaves.bit_length()):
        reach = jnp.where((q + 1) % (2 ** (bit + 1)) == 0, 2 ** (bit + 1), reach)
    upper = (q // (2 * reach)) % 2 == 1
    parent = jnp.where(upper, q - reach, q + reach)
    low_child = q - reach // 2
    high_child = q + reach // 2
    climbs = node & jnp.logical_not(joint)
    inner = node & jnp.logical_not(fourth)

    def over(plane):
        return (4 * plane + place, c)

    def in_plane(dc, dx, dy):
        return (4 * q + 2 * ((b1 + dy) % 2) + (b0 + dx) % 2, (c + dc) % 2)

    def when(cond, action):
        if cond is None:
            action()
        else:
            @pl.when(cond)
            def _():
                action()

    others = [(dc, dx, dy) for dx in range(2) for dy in range(2) for dc in range(2) if (dc, dx, dy) != (0, 0, 0)]
    peers = [(None, in_plane(*other)) for other in others] + [
        (None, over(pair_plane)),
        (fourth, over(q + 1)),
        (q % 4 == 2, over(q - 1)),
        (fourth, over(q + 2)),
        (q % 4 == 3, over(q - 2)),
        (climbs, over(parent)),
        (inner, over(low_child)),
        (inner, over(high_child)),
        (last, over(below_top)),
        (joint, over(planes - 1)),
    ]
    barrier = pltpu.get_barrier_semaphore()
    expected = 0
    for cond, to in peers:
        when(cond, lambda to=to: pl.semaphore_signal(barrier, inc=1, device_id=to, device_id_type=pl.DeviceIdType.MESH))
        expected = expected + (1 if cond is None else jnp.where(cond, 1, 0))

    own_cols = pl.ds(pl.multiple_of(c * part, part), part)
    other_cols = pl.ds(pl.multiple_of(oc * part, part), part)
    loads = []
    for src, dst in (
        (sinv_hbm.at[0], sinv),
        (scpl_hbm.at[0], scpl),
        (rhs_hbm.at[0], rhs),
        (srhs_hbm.at[0], srhs),
        (inv_hbm.at[0, :, own_cols], inv.at[:, own_cols]),
        (inv_hbm.at[0, :, other_cols], inv.at[:, other_cols]),
        (couple_hbm.at[0], couple),
    ):
        copy = pltpu.make_async_copy(src, dst, load_sem.at[len(loads)])
        copy.start()
        loads.append(copy)

    pending = []
    names = {}

    def sem(*name):
        return recv_sem.at[names.setdefault(name, len(names))]

    def remote(src, dst, rsem, to):
        return pltpu.make_async_remote_copy(
            src_ref=src, dst_ref=dst, send_sem=send_sem.at[0], recv_sem=rsem,
            device_id=to, device_id_type=pl.DeviceIdType.MESH,
        )

    def push(src, dst, rsem, to, cond=None):
        copy = remote(src, dst, rsem, to)
        when(cond, lambda: copy.start())
        pending.append((cond, copy))

    def arrive(dst, rsem, cond=None):
        copy = remote(dst, dst, rsem, mate)
        when(cond, lambda: copy.wait_recv())

    loads[0].wait()
    loads[1].wait()

    @pl.when(is_top)
    def _():
        parts[0] = three_pass(sinv[...], sinv[...], dot_tn).reshape(2, half, width)

    @pl.when(jnp.logical_not(is_top))
    def _():
        parts[0] = three_pass(scpl[...], sinv[...], dot_nn).reshape(2, half, width)

    loads[2].wait()
    loads[3].wait()
    with scope("barrier"):
        pl.semaphore_wait(barrier, expected)

    push(parts.at[0, oc], part_in.at[0], sem("part", 0), mate)
    push(rhs, other_rhs, sem("rhs"), mate)

    for k in range(2):
        for h in range(2):
            sem("rb", k, h)
    for dc, dx, dy in others:
        to = in_plane(dc, dx, dy)
        block = to[1] * 4 + (to[0] % 4) % 2 * 2 + (to[0] % 4) // 2
        push(
            srhs.at[pl.ds(pl.multiple_of(block * eighth, eighth), eighth)], rb.at[b1, c],
            recv_sem.at[names[("rb", 0, 0)] + 2 * b1 + c], to, right,
        )
    block8 = c * 4 + b0 * 2 + b1

    @pl.when(right)
    def _():
        rb[b1, c] = srhs[pl.ds(pl.multiple_of(block8 * eighth, eighth), eighth), :]

    push(srhs.at[pl.ds(pl.multiple_of(oc * mid, mid), mid)], srows.at[c], sem("srows"), mate, left)

    @pl.when(left)
    def _():
        srows[c] = srhs[pl.ds(pl.multiple_of(c * mid, mid), mid), :]

    parts[1] = three_pass(sinv[...], sinv[...], dot_tn).reshape(2, half, width)
    push(parts.at[1, oc], part_in.at[1], sem("part", 1), mate)

    loads[4].wait()
    piece = part // 4
    for j in range(4):
        at_j = pl.ds(j * piece, piece)
        leaf_out[:, at_j] = dot_nt(rhs[...], inv[at_j, own_cols])

    own = b0 * (1 + b1)
    theirs = (1 - b0) * (1 + b1)
    across = 2 - b1
    paired = 2 + q % 2

    def spot(kind, idx, core, i):
        return fac.at[kind, idx, core, pl.ds(i * chunk, chunk)]

    def share_up(kind, idx, i, cond):
        push(spot(kind, idx, c, i), spot(kind, 3, c, i), sem("z", kind, i // 2), over(pair_plane), even_plane & cond)
        if kind == 0:
            push(
                spot(kind, idx, c, i), top.at[c, pl.ds(i * chunk, chunk)], sem("top"), over(below_top), last & cond,
            )

    def own_x(kind, chunks, cond=None):
        for i in chunks:
            push(spot(kind, own, c, i), spot(kind, own, c, i), sem("x", kind, i), (xp, c), cond)

    def own_y(kind, chunks):
        for i in chunks:
            push(spot(kind, own, c, i), spot(kind, own, c, i), sem("y", kind, i), (yp, c), right)
            share_up(kind, own, i, right & far)

    def own_mate(kind):
        push(fac.at[kind, own, c], fac.at[kind, own, c], sem("own", kind), mate)

    def relay_x(kind, chunks=range(CHUNKS)):
        for i in chunks:
            arrive(spot(kind, theirs, c, i), sem("x", kind, i))
            push(spot(kind, theirs, c, i), spot(kind, theirs, c, i), sem("y", kind, i), (yp, c), left)
            push(spot(kind, theirs, c, i), spot(kind, theirs, c, i), sem("theirs", kind), mate)
            share_up(kind, theirs, i, left & far)

    def relay_y(kind, cond=None):
        for i in range(CHUNKS):
            arrive(spot(kind, across, c, i), sem("y", kind, i), cond)
            push(spot(kind, across, c, i), spot(kind, across, c, i), sem("across", kind), mate, cond)
            share_up(kind, across, i, near if cond is None else near & cond)

    def relay_z(kind):
        for k in range(2):
            span = pl.ds(k * half // 2, half // 2)
            arrive(fac.at[kind, 3, c, span], sem("z", kind, k), odd_plane)
            push(fac.at[kind, 3, c, span], fac.at[kind, 3, c, span], sem("paired", kind), mate, odd_plane)

    def whole(kind, which):
        idx = {"own": own, "theirs": theirs, "across": across, "paired": 3}[which]
        arrive(fac.at[kind, idx, oc], sem(which, kind), odd_plane if which == "paired" else None)

    def factor(kind, idx):
        return fac[kind, idx].reshape(width, width)

    with scope("part0"):
        arrive(part_in.at[0], sem("part", 0))
    fac[0, own, c] = (parts[0, c] + part_in[0]).astype(BF16)
    own_x(0, range(CHUNKS), left)
    own_x(0, range(CHUNKS - 1), right)
    own_y(0, range(CHUNKS))
    own_mate(0)

    with scope("rhs"):
        arrive(other_rhs, sem("rhs"))
    loads[5].wait()
    for j in range(4):
        at_j = pl.ds(j * piece, piece)
        state[:, at_j] = (leaf_out[:, at_j] + dot_nt(other_rhs[...], inv[at_j, other_cols])).astype(BF16)
    loads[6].wait()
    out_send[...] = dot_nt(state[pl.ds(pl.multiple_of(oc * mid, mid), mid), :], couple[...])
    push(out_send, out_in, sem("out"), mate)
    out_own[...] = dot_nt(state[pl.ds(pl.multiple_of(c * mid, mid), mid), :], couple[...])

    arrive(part_in.at[1], sem("part", 1))
    fac[1, own, c] = (parts[1, c] + part_in[1]).astype(BF16)
    own_mate(1)

    arrive(srows.at[oc], sem("srows"), left)
    with scope("out"):
        arrive(out_in, sem("out"))
    given = jnp.where(left, jnp.concatenate([srows[0], srows[1]], axis=1), 0.0)
    base[...] = (given - (out_own[...] + out_in[...])).reshape(2, quarter, width)
    xs[...] = base[1 - b0].astype(BF16)
    push(xs, xr, sem("xr"), (xp, c))
    own_x(0, range(CHUNKS - 1, CHUNKS), right)
    own_x(1, range(CHUNKS))
    own_y(1, range(2))

    with scope("relay_x0"):
        relay_x(0)
    with scope("relay_y0"):
        relay_y(0, right)
    with scope("xr"):
        arrive(xr, sem("xr"))
    with scope("m1"):
        whole(0, "own")
        whole(0, "theirs")
    w1s[...] = base[b0] + xr[...].astype(F32)
    o1[...] = two_pass(-w1s[...], factor(0, 0), dot_nt).reshape(2, eighth, width)
    ys[...] = o1[1 - b1].astype(BF16)
    push(ys, yr, sem("yr"), (yp, c))
    own_y(1, range(2, CHUNKS))
    with scope("relay_y0"):
        relay_y(0, left)

    for k in range(2):
        for h in range(2):
            arrive(rb.at[k, h], sem("rb", k, h), jnp.logical_not(right & (b1 == k) & (c == h)))
    push(rb.at[1], rp, sem("rp"), over(pair_plane), even_plane)
    push(rb.at[1], rt, sem("rt"), over(below_top), last)
    with scope("m2"):
        whole(0, "across")
    with scope("yr"):
        arrive(yr, sem("yr"))
    w2s[...] = jnp.concatenate([rb[0, 0], rb[0, 1]], axis=1) + (o1[b1] + yr[...].astype(F32))
    out2 = two_pass(w2s[...], factor(0, 1), dot_nt)
    zb[0] = out2.astype(BF16)
    zb_own = w3s
    zb_own[...] = out2
    push(zb.at[0], zr.at[0], sem("zr", 0), over(pair_plane))

    with scope("relay_z0"):
        relay_z(0)
    with scope("relay_x1"):
        relay_x(1)
    arrive(rp, sem("rp"), odd_plane)
    with scope("zr0"):
        arrive(zr.at[0], sem("zr", 0))
    with scope("m3"):
        whole(0, "paired")
    given = jnp.where(
        even_plane, jnp.concatenate([rb[1, 0], rb[1, 1]], axis=1), jnp.concatenate([rp[0], rp[1]], axis=1)
    )
    w3s[...] = given - (w3s[...] + zr[0].astype(F32))
    out3 = two_pass(w3s[...], factor(0, paired), dot_nt)
    zb[1] = out3.astype(BF16)
    st[...] = out3
    push(zb.at[1], zr.at[1], sem("zr", 1), over(q - 1), q % 4 == 2)

    with scope("relay_y1"):
        relay_y(1)

    sem("zr", 2)
    arrive(zr.at[2], sem("zr", 2), inner)
    with scope("zr1"):
        arrive(zr.at[1], sem("zr", 1), node)

    @pl.when(node)
    def _():
        first = jnp.where(fourth, st[...], zr[2].astype(F32))
        w4s[...] = jnp.concatenate([rb[1, 0], rb[1, 1]], axis=1) - (first + zr[1].astype(F32))
        out4 = two_pass(w4s[...], factor(0, 2), dot_nt)
        st[...] = out4
        zb[2] = out4.astype(BF16)

    up = jnp.where(upper, 1, 2)
    push(
        zb.at[2], zr.at[up], recv_sem.at[jnp.where(upper, names[("zr", 1)], names[("zr", 2)])], over(parent), climbs,
    )
    arrive(top.at[c], sem("top"), joint)
    push(top.at[c], top.at[c], sem("top_mate"), mate, joint)
    arrive(rt, sem("rt"), joint)
    with scope("n3"):
        for which in ("own", "theirs", "across"):
            whole(1, which)
    arrive(top.at[oc], sem("top_mate"), joint)

    @pl.when(joint)
    def _():
        wt = jnp.concatenate([rt[0], rt[1]], axis=1) - st[...]
        st[...] = two_pass(wt, top[...].reshape(width, width), dot_nn)

    with scope("dn1"):
        arrive(dn.at[1], sem("dn", 1), climbs)

    @pl.when(node)
    def _():
        above = jnp.where(joint, st[...], dn[1].astype(F32))
        s4[...] = two_pass(w4s[...], factor(1, 2), dot_nn) - two_pass(above, factor(0, 2), dot_nn)
        sb[...] = s4[...].astype(BF16)

    for plane in (q - 1, q + 1, q + 2):
        push(sb, dn.at[0], sem("dn", 0), over(plane), fourth)
    for plane in (low_child, high_child):
        push(sb, dn.at[1], sem("dn", 1), over(plane), inner)
    push(st, sols, sem("top_back"), over(planes - 1), joint)

    w1n = two_pass(w1s[...], factor(1, 0), dot_nn)
    slot = c * 2 + b0
    w1g[slot] = w1n.astype(BF16)
    for dc, dx in ((1, 0), (0, 1), (1, 1)):
        push(w1g.at[slot], w1g.at[slot], sem("w1n", dc, dx), in_plane(dc, dx, 0))
    w2s[...] = two_pass(w2s[...], factor(1, 1), dot_nn)
    with scope("relay_z1"):
        relay_z(1)
        whole(1, "paired")
    w3s[...] = two_pass(w3s[...], factor(1, paired), dot_nn)

    with scope("dn0"):
        arrive(dn.at[0], sem("dn", 0), jnp.logical_not(fourth))
    above3 = jnp.where(fourth, sb[...], dn[0])
    s3[...] = w3s[...] - dot_nn(above3, factor(0, paired))
    s2[...] = w2s[...] - dot_nn(s3[...].astype(BF16), factor(0, 1))
    sg[block8] = s2[...].astype(BF16)
    for dx, dy, dc in ((1, 0, 0), (0, 1, 0), (1, 0, 1), (0, 1, 1), (1, 1, 0), (1, 1, 1), (0, 0, 1)):
        push(sg.at[block8], sg.at[block8], sem("sg", dc, dx, dy), in_plane(dc, dx, dy))

    def deliver(src, to, cond):
        for h in range(2):
            cols = pl.ds(h * half, half)
            here = (p == to) & (c == h)
            push(src.at[:, cols], sep_acc.at[block8], sem("acc"), (to, h), cond & jnp.logical_not(here))

            @pl.when(here & cond)
            def _():
                sep_acc[block8] = src[:, cols]

    def backward(group, side):
        spans = [
            pl.ds(pl.multiple_of(t * quarter + side * eighth, eighth), eighth) for t in range(4)
        ]
        inside = pl.ds(pl.multiple_of(side * eighth, eighth), eighth)
        above = jnp.concatenate([sg[2 * t + side] for t in range(4)], axis=0)
        free = jnp.concatenate([w1g[t, inside] for t in range(4)], axis=0).astype(F32)
        sol1 = free - dot_nn(above, factor(0, 0))

        @pl.when(left)
        def _():
            mine = jnp.where(c == 0, sol1[:, :half], sol1[:, half:])
            for t in range(4):
                sep_out[spans[t], :] = mine[t * eighth:(t + 1) * eighth]

        before = jnp.concatenate([state[span, :] for span in spans], axis=0).astype(F32)
        residue = (before - dot_nn(sol1.astype(BF16), couple[...])).astype(BF16)
        for j in range(4):
            cols = pl.ds(pl.multiple_of(oc * part + j * piece, piece), piece)
            fin_s[group, j] = dot_nn(residue, inv[:, cols]).astype(BF16)
            push(fin_s.at[group, j], fin_r.at[group, j], sem("fin", group, j), mate)
        for j in range(4):
            cols = pl.ds(pl.multiple_of(c * part + j * piece, piece), piece)
            value = dot_nn(residue, inv[:, cols])
            for t in range(4):
                leaf_out[spans[t], pl.ds(j * piece, piece)] = value[t * eighth:(t + 1) * eighth]
        return spans

    def gathered(dc, dx, dy):
        block = ((c + dc) % 2) * 4 + ((b0 + dx) % 2) * 2 + (b1 + dy) % 2
        arrive(sg.at[block], sem("sg", dc, dx, dy))

    with scope("w1n"):
        for dc, dx in ((1, 0), (0, 1), (1, 1)):
            arrive(w1g.at[((c + dc) % 2) * 2 + (b0 + dx) % 2], sem("w1n", dc, dx))
    with scope("sg0"):
        gathered(1, 0, 0)
        gathered(0, 1, 0)
        gathered(1, 1, 0)
    spans = [backward(0, b1)]
    with scope("sg1"):
        for dc, dx in ((0, 0), (1, 0), (0, 1), (1, 1)):
            gathered(dc, dx, 1)
    always = q >= 0
    deliver(s2, 4 * q + 1, always)
    deliver(s3, 4 * q + 3, even_plane)
    deliver(s4, 4 * q + 3, node)
    arrive(sols, sem("top_back"), last)
    deliver(sols, 4 * q + 3, last)
    spans.append(backward(1, 1 - b1))
    with scope("fin"):
        for group in range(2):
            for j in range(4):
                arrive(fin_r.at[group, j], sem("fin", group, j))
                for t in range(4):
                    leaf_out[spans[group][t], pl.ds(j * piece, piece)] += fin_r[
                        group, j, pl.ds(t * eighth, eighth)
                    ].astype(F32)

    with scope("acc"):
        arrive(sep_acc.at[pl.ds(0, 7)], sem("acc"), right)

    @pl.when(right)
    def _():
        sep_out[...] = sep_acc[...].reshape(rows, half)

    with scope("drain"):
        for cond, copy in pending:
            when(cond, lambda copy=copy: copy.wait_send())
    assert len(names) == RECEIVES, len(names)


def local(leaves, leaf_rhs, leaf_inv, leaf_couple, sep_rhs, sep_inv, sep_couple):
    _, rows, part = leaf_rhs.shape
    full = leaf_inv.shape[2]
    width = sep_inv.shape[2]
    half = width // 2
    mid, quarter, eighth = rows // 2, rows // 4, rows // 8
    vmem = pl.BlockSpec(memory_space=pltpu.VMEM)
    anywhere = pl.BlockSpec(memory_space=pl.ANY)
    V = pltpu.VMEM
    dma = pltpu.SemaphoreType.DMA
    leaf_solution, sep_solution = pl.pallas_call(
        functools.partial(kernel, leaves),
        out_shape=(pltpu.VMEM((rows, part), F32), pltpu.VMEM((rows, half), F32)),
        in_specs=[anywhere] * 6,
        out_specs=(vmem, vmem),
        scratch_shapes=[
            V((rows, part), BF16), V((part, full), BF16), V((width, part), BF16), V((rows, half), F32),
            V((half, width), F32), V((width, half), F32), V((rows, part), BF16), V((rows, part), BF16),
            V((2, 2, half, width), F32), V((2, half, width), F32), V((2, 4, 2, half, width), BF16),
            V((2, half, width), BF16), V((2, mid, half), F32), V((2, 2, eighth, half), F32),
            V((2, eighth, half), F32), V((2, eighth, half), F32),
            V((mid, width), F32), V((mid, width), F32), V((mid, width), F32), V((2, quarter, width), F32),
            V((quarter, width), BF16), V((quarter, width), BF16), V((quarter, width), F32),
            V((2, eighth, width), F32), V((eighth, width), BF16), V((eighth, width), BF16),
            V((3, eighth, width), BF16), V((3, eighth, width), BF16), V((eighth, width), F32),
            V((eighth, width), F32), V((eighth, width), F32), V((eighth, width), F32), V((eighth, width), BF16),
            V((2, eighth, width), BF16), V((4, quarter, width), BF16), V((8, eighth, width), BF16),
            V((eighth, width), F32), V((eighth, width), F32), V((eighth, width), F32), V((eighth, width), F32),
            V((2, 4, mid, part // 4), BF16), V((2, 4, mid, part // 4), BF16), V((8, eighth, half), F32),
            dma((7,)), dma((1,)), dma((RECEIVES,)),
        ],
        compiler_params=pltpu.CompilerParams(
            collective_id=0, has_side_effects=True, vmem_limit_bytes=60 * 1024 * 1024
        ),
    )(leaf_rhs, leaf_inv, leaf_couple, sep_rhs, sep_inv, sep_couple)
    return leaf_solution[None], sep_solution[None]


def solution(mesh):
    return jax.shard_map(
        functools.partial(local, mesh.shape["leaf"]),
        mesh=mesh,
        in_specs=(
            P("leaf", None, "sep"),
            P("leaf", "sep", None),
            P("leaf", None, "sep"),
            P("leaf", None, "sep"),
            P("leaf", "sep", None),
            P("leaf", None, "sep"),
        ),
        out_specs=(P("leaf", None, "sep"), P("leaf", None, "sep")),
        check_vma=False,
    )
```

time: 51.3 us -> 47.7 us (0.930); the launches traced: 50.3 us -> 47.3 us
  Pallas kernels: 48 us -> 45 us
    pallas_call x1, Pallas kernels: 48 us -> 45 us  [local(): pl.pallas_call(functools.partial(kernel, leaves), out_shape=(pltpu.VMEM((...]
where the time goes in v1:
time: 47.7 us; the launch traced here: 47.3 us
  Pallas kernels  45 us (94%)
  local copies, waits for them, and re-layouts  1.67 us (4%)
  between operations  0.64 us (1%)
    pallas_call x1, Pallas kernels, local(): pl.pallas_call(functools.partial(kernel, leaves), out_shape=(pltpu.VMEM((...  45 us
    unnamed x2, local copies, waits for them, and re-layouts  1.67 us

profile of v1, /device:TPU:31, one launch (start us, length us, event | category | flops | bytes accessed | tf_op | source)
XLA Modules:
  0.0 47.3 jit_solution(5082108187395228872)
XLA Ops:
  0.6 45.0 %shard_map.77 = (f32[256,1024]{1,0:T(8,128)S(1)}, f32[256,256]{1,0:T(8,128)S(1)}) custom-call(bf16[1,256,1024]{2,1,0:T(8,128)(2,1)} %rhs_hbm.1, bf16[1,1024,2048]{2,1,0:T(8,128)(2,1)} %inv_hbm.1, bf16[1,512,1024]{2,1,0:T(8,128)(2,1)} %couple_hbm.1, f32[1,256,256]{2,1,0:T(8,128)} %srhs_hbm.1, f32[1,256,512]{2,1,0:T(8,128)} %sinv_hbm.1, f32[1,512,256]{2,1,0:T(8,128)} %scpl_hbm.1), custom_call_target="tpu_custom_call" | custom-call | tf_op jit(solution)/shard_map/pallas_call | solution.py:519
  45.6 1.0 %copy.10 = f32[1,256,1024]{2,1,0:T(8,128)} copy(f32[1,256,1024]{2,1,0:T(8,128)S(1)} %bitcast.2) | data formatting | bytes 2097152
  46.6 0.7 %copy.11 = f32[1,256,256]{2,1,0:T(8,128)} copy(f32[1,256,256]{2,1,0:T(8,128)S(1)} %bitcast.3) | data formatting | bytes 524288
